TPU v7x, 32 devices: a whole 2x2x4 slice. The times are simulated.
32 devices in a mesh: dp: 16 (over z, y, x), head: 2 (over core).
Axes of the slice: x: 2, y: 2, z: 4, core: 2. Of those that a mesh axis runs over, the one named last changes fastest.
Arguments:
- hidden: bfloat16 [64, 512, 3584], P(('dp', 'head')), may hold values from -6 to 6
- head_proj: bfloat16 [4, 3584, 128], P('head'), may hold values from -0.09375 to 0.09375
- head_out: bfloat16 [4, 128], P('head'), may hold values from -0.8984375 to 0.8984375
- head_ratio: int32 [4], replicated, may hold values from 2 to 7
- group_of: int32 [64], replicated, may hold values from 0 to 3, as said below
- lengths: int32 [64], P(('dp', 'head')), may hold values from 1 to 512
- token_mask: int32 [64, 512], P(('dp', 'head')), may hold values 0 or 1
Outputs:
- advantages: float32 [64, 512], P(('dp', 'head'))
Inputs may be any that keep to these rules, and one draw needn't show every extreme that they name: `group_of`: every one of the 4 groups holds exactly 16 rollouts.
All inputs are finite; a program needn't handle non-finite values. No bound on the sum of `token_mask` on one device may be relied on, other than what follows from the above.
Results may differ from a plain program's by a relative error of at most 0.0026.
Values may be sent and summed in bfloat16 or wider, within the bound.
A program may use at most 64 MiB of HBM per device.

v0:
```python
import jax
import jax.numpy as jnp
from jax import lax
from jax.sharding import PartitionSpec as P

GROUP = 16


token_weight = 0.5
gap_weight = 0.5
clip_limit = 2.0
var_offset = 0.04


def head_mixture(head_ratio):
    ratios = head_ratio.astype(jnp.float32)
    return ratios / jnp.sum(ratios)


def mixture_scores(states, projection, readout, mix_weights):
    count_rows, seq_len, model_width = states.shape
    flat_rows = states.reshape(count_rows * seq_len, model_width)
    hidden_pre = jnp.einsum(
        "td,hdr->htr", flat_rows, projection, preferred_element_type=jnp.float32
    )
    active = jnp.tanh(hidden_pre).astype(jnp.bfloat16)
    scores = jnp.einsum("htr,hr->ht", active, readout, preferred_element_type=jnp.float32)
    return jnp.sum(mix_weights[:, None] * scores, axis=0).reshape(count_rows, seq_len)


def on_device(hidden, head_proj, head_out, head_ratio, group_of, lengths, token_mask):
    rollouts, seq_len, model_width = hidden.shape
    mixture = head_mixture(head_ratio)
    combined = mixture_scores(
        hidden,
        lax.all_gather(head_proj, "head", axis=0, tiled=True),
        lax.all_gather(head_out, "head", axis=0, tiled=True),
        mixture,
    )
    positions = jnp.arange(seq_len)
    last_mark = positions[None, :] == (lengths - 1)[:, None]
    reward = jnp.sum(jnp.where(last_mark, combined, 0.0), axis=1)
    group_count = group_of.shape[0] // GROUP
    labels = jnp.arange(group_count)
    start_row = lax.axis_index(("dp", "head")) * rollouts
    my_groups = lax.dynamic_slice_in_dim(group_of, start_row, rollouts)
    member = (my_groups[:, None] == labels[None, :]).astype(jnp.float32)
    everyone = lax.all_gather(reward, ("dp", "head"), axis=0, tiled=True)
    whole_member = (group_of[:, None] == labels[None, :]).astype(jnp.float32)
    group_mean = jnp.sum(whole_member * everyone[:, None], axis=0) / GROUP
    whole_dev = everyone - jnp.sum(whole_member * group_mean[None, :], axis=1)
    group_var = jnp.sum(whole_member * (whole_dev * whole_dev)[:, None], axis=0) / GROUP
    group_best = jnp.max(jnp.where(whole_member > 0, everyone[:, None], -jnp.inf), axis=0)
    mean_rows = jnp.sum(member * group_mean[None, :], axis=1)
    deviation = reward - mean_rows
    var_rows = jnp.sum(member * group_var[None, :], axis=1)
    best_rows = jnp.sum(member * group_best[None, :], axis=1)
    shaped = (
        (deviation / jnp.sqrt(var_rows + var_offset))[:, None]
        + token_weight * combined
        - gap_weight * (best_rows - reward)[:, None]
    )
    valid_mask = (positions[None, :] < lengths[:, None]) & (token_mask == 1)
    return jnp.where(valid_mask, jnp.clip(shaped, -clip_limit, clip_limit), 0.0)


def solution(mesh):
    return jax.shard_map(
        on_device,
        mesh=mesh,
        in_specs=(
            P(("dp", "head"), None, None),
            P("head", None, None),
            P("head", None),
            P(),
            P(),
            P(("dp", "head")),
            P(("dp", "head"), None),
        ),
        out_specs=P(("dp", "head"), None),
        check_vma=False,
    )
```

profile of v0, /device:TPU:0, one launch (start us, length us, event | category | flops | bytes accessed | tf_op | source)
XLA Modules:
  0.0 82.1 jit_solution(8619927760031545544)
XLA Ops:
  6.5 0.0 all-gather.3.cloned.1.call-start
  6.5 0.7 all-gather.3.cloned.1.call-update
  7.3 0.7 dynamic_slice.3
  8.0 2.1 %all-gather = bf16[2,2,128]{2,1,0:T(2,128)(2,1)S(1)} all-gather(bf16[1,2,128]{2,1,0:T(2,128)(2,1)} %bitcast.14), channel_id=1, replica_groups=mesh['dp'=16,'head'=2] {'head'}, dimensions={0}, use_global_device_ids=true | all-gather | bytes 1536 | tf_op jit(solution)/shard_map/all_gather | solution.py:37
  10.1 1.3 %convert_reduce_fusion = f32[]{:T(128)} fusion(s32[4]{0:T(128)} %param.10), kind=kLoop, calls=%fused_computation.22 | loop fusion | flops 7 | bytes 20 | tf_op jit(solution)/shard_map/reduce_sum | solution.py:17
  11.3 1.3 %convert_divide_fusion = f32[4]{0:T(128)S(1)} fusion(s32[4]{0:T(128)} %param.10, f32[]{:T(128)} %convert_reduce_fusion), kind=kLoop, calls=%fused_computation.21 | loop fusion | flops 8 | bytes 36 | tf_op jit(solution)/shard_map/div | solution.py:17
  12.6 0.7 broadcast_add_fusion
  13.3 11.2 %all-gather.3.cloned.1.call-done = bf16[4,3584,128]{2,1,0:T(8,128)(2,1)} async-done(((bf16[2,3584,128]{2,1,0:T(8,128)(2,1)}), bf16[4,3584,128]{2,1,0:T(8,128)(2,1)}) %all-gather.3.cloned.1.call-update) | async-done | bytes 3670032 | tf_op jit(solution)/shard_map/all_gather | solution.py:36
  24.5 0.0 copy-start.2
  24.5 0.0 copy-start
  24.5 0.0 copy-start.1
  24.5 8.4 %fusion = f32[4,1,1024]{2,1,0:T(1,128)S(1)} fusion(bf16[4,3584,128]{2,1,0:T(8,128)(2,1)} %all-gather.3.cloned.1.call-done, bf16[1024,3584,1]{1,0,2:T(8,128)(2,1)} %bitcast.13, bf16[4,128,1]{1,0,2:T(4,128)(2,1)S(1)} %bitcast.15), kind=kOutput, calls=%fused_computation.1 | convolution fusion | flops 3759669248 | bytes 11027456 | tf_op jit(solution)/shard_map/htr,hr->ht/dot_general | solution.py:27
  32.9 0.1 fusion.1
  33.0 0.2 fusion.2
  33.2 0.2 dynamic-update-slice
  33.5 40.5 %all-reduce = f32[64]{0:T(128)S(1)} all-reduce(f32[64]{0:T(128)S(1)} %dynamic-update-slice), channel_id=1, replica_groups=mesh['dp'=16,'head'=2] {'dp','head'}, use_global_device_ids=true, to_apply=%add | all-reduce | flops 64 | bytes 512
  74.0 0.0 copy-done.2
  74.0 0.1 select_reduce_fusion.3
  74.1 0.1 select_reduce_fusion.2
  74.2 0.1 select_reduce_fusion.1
  74.3 0.2 select_reduce_fusion.6
  74.6 0.0 copy-done
  74.6 0.0 copy-done.1
  74.6 0.7 and_select_fusion
  (6 shorter events, 0.0 us)
Async XLA Ops:
  6.5 18.0 %all-gather.3.cloned.1.call-start = ((), (), s32[]{:S(2)}) async-start(), calls=%async_computation | async-start | bytes 5505024 | tf_op jit(solution)/shard_map/all_gather | solution.py:36
  24.5 49.4 %copy-start.2 = (s32[64]{0:T(128)S(1)}, s32[64]{0:T(128)}, u32[]{:S(2)}) copy-start(s32[64]{0:T(128)} %param.11) | copy-start | bytes 772
  24.5 50.0 %copy-start = (s32[2,512]{1,0:T(2,128)S(1)}, s32[2,512]{1,0:T(2,128)}, u32[]{:S(2)}) copy-start(s32[2,512]{1,0:T(2,128)} %param.13) | copy-start | bytes 12292
  24.5 50.0 %copy-start.1 = (s32[2]{0:T(128)S(1)}, s32[2]{0:T(128)}, u32[]{:S(2)}) copy-start(s32[2]{0:T(128)} %param.12) | copy-start | bytes 28
Sparse Core Ops, SparseCore 0:
  8.9 15.6 all-gather.2
where the time goes:
time: 82.4 us; the launch traced here: 82.1 us
  blocking collectives  42.5 us (52%)
  between operations  13.4 us (16%)
  waiting for transfers between devices  11.9 us (14%)
  matrix products  8.41 us (10%)
  other arithmetic  4.75 us (6%)
  local copies, waits for them, and re-layouts  0.99 us (1%)
    unnamed x1, blocking collectives  40.5 us
    all_gather x1, waiting for transfers between devices, on_device(): lax.all_gather(head_proj, 'head', axis=0, tiled=True)  11.2 us
    dot_general x1, matrix products, mixture_scores(): jnp.einsum('htr,hr->ht', active, readout, preferred_element_type=jnp.floa...  8.41 us
    all_gather x1, blocking collectives, on_device(): lax.all_gather(head_out, 'head', axis=0, tiled=True)  2.08 us
  transfers between devices with their start and end apart: 1, of which 1 were waited for; matrix products, arithmetic and copies ran while one was open for 5% of the time, Pallas kernels for 0%

commit v1 on v0

v1 whole, which is shorter than its diff:
```python
import functools

import jax
import jax.numpy as jnp
from jax import lax
from jax.experimental import pallas as pl
from jax.experimental.pallas import tpu as pltpu
from jax.sharding import PartitionSpec as P

GROUP = 16
MESH = pl.DeviceIdType.MESH

token_weight = 0.5
gap_weight = 0.5
clip_limit = 2.0
var_offset = 0.04

ROW_PIECES = 4
DEPTH_PIECES = 2
PACK = 16


def kernel(
    chips,
    hidden, proj, readout, ratio, groups, lens, mask, out,
    rows_all, w_own, w_other, out_own, out_other, acc, comb, ends, msg, slots,
    ratio_s, groups_s, lens_s, groups_v, mask_v,
    row_sem, w_sem, small_sem, pair_send, pair_recv, all_send, all_recv,
):
    chip, core = lax.axis_index("dp"), lax.axis_index("head")
    width = hidden.shape[2]
    count, seq = mask.shape
    heads, _, rank = proj.shape
    devices = 2 * chips
    me = 2 * chip + core
    total_rows = count * seq
    piece = total_rows // ROW_PIECES
    blocks = piece // PACK
    depth = width // DEPTH_PIECES
    lanes = msg.shape[1]

    loads = [pltpu.make_async_copy(lens, lens_s, small_sem.at[0])]
    loads.append(pltpu.make_async_copy(ratio, ratio_s, small_sem.at[1]))
    loads.append(pltpu.make_async_copy(groups, groups_s, small_sem.at[2]))
    loads.append(pltpu.make_async_copy(readout, out_own, small_sem.at[3]))
    loads.append(pltpu.make_async_copy(groups, groups_v.at[0], small_sem.at[4]))
    loads.append(pltpu.make_async_copy(mask, mask_v, small_sem.at[5]))
    w_loads = [
        pltpu.make_async_copy(proj.at[k], w_own.at[:, pl.ds(k * rank, rank)], w_sem.at[k])
        for k in range(heads)
    ]
    h_loads = [
        pltpu.make_async_copy(
            hidden.at[pl.ds(m * blocks, blocks)],
            rows_all.at[pl.ds(m * blocks, blocks)],
            row_sem.at[m],
        )
        for m in range(ROW_PIECES)
    ]
    for copy in w_loads + h_loads + loads:
        copy.start()

    barrier = pltpu.get_barrier_semaphore()

    def greet(step, _):
        other = lax.rem(me + step, devices)
        pl.semaphore_signal(
            barrier, inc=1, device_id=(other // 2, lax.rem(other, 2)), device_id_type=MESH
        )
        return 0

    lax.fori_loop(1, devices, greet, 0)

    for copy in loads + w_loads:
        copy.wait()

    weights = [ratio_s[k].astype(jnp.float32) for k in range(2 * heads)]
    weight_sum = sum(weights[1:], weights[0])
    own_mix = [
        ratio_s[core * heads + k].astype(jnp.float32) / weight_sum for k in range(heads)
    ]
    other_mix = [
        ratio_s[(1 - core) * heads + k].astype(jnp.float32) / weight_sum for k in range(heads)
    ]

    def reader(values):
        wide = values[...].astype(jnp.float32)
        line = lax.broadcasted_iota(jnp.int32, (8, rank), 0)
        parts = [
            jnp.where(line == k, jnp.broadcast_to(wide[k : k + 1], (8, rank)), 0.0)
            for k in range(heads)
        ]
        return jnp.concatenate(parts, axis=1).astype(jnp.bfloat16)

    def scores(inner, lhs, mix):
        active = jnp.tanh(inner).astype(jnp.bfloat16)
        per_head = lax.dot_general(
            lhs, active, (((1,), (1,)), ((), ())), preferred_element_type=jnp.float32
        )
        line = mix[0] * per_head[0:1]
        for k in range(1, heads):
            line = line + mix[k] * per_head[k : k + 1]
        return line

    own_lhs = reader(out_own)

    def rows_of(m, cut):
        return rows_all[pl.ds(m * blocks, blocks), :, cut].reshape(piece, -1)

    def own_piece(m):
        at = pl.ds(m * piece, piece)
        inner = jnp.dot(rows_of(m, pl.ds(0, width)), w_own[...], preferred_element_type=jnp.float32)
        comb[:, at] = scores(inner, own_lhs, own_mix)

    for m in range(ROW_PIECES - 1):
        h_loads[m].wait()
        own_piece(m)
    h_loads[ROW_PIECES - 1].wait()

    sub = lax.broadcasted_iota(jnp.int32, (PACK, width), 0)
    picked = jnp.zeros((PACK, width), jnp.float32)
    for r in range(count):
        last = lens_s[r] - 1
        block = rows_all[r * (seq // PACK) + lax.div(last, PACK)].astype(jnp.float32)
        row = jnp.sum(jnp.where(sub == lax.rem(last, PACK), block, 0.0), axis=0, keepdims=True)
        picked = jnp.where(sub == r, jnp.broadcast_to(row, (PACK, width)), picked)
    ends[pl.ds(0, PACK), :] = picked.astype(jnp.bfloat16)

    pl.semaphore_wait(barrier, devices - 1)

    def to_pair(src, dst, k):
        return pltpu.make_async_remote_copy(
            src_ref=src, dst_ref=dst, send_sem=pair_send.at[k], recv_sem=pair_recv.at[k],
            device_id=(chip, 1 - core), device_id_type=MESH,
        )

    send_ends = to_pair(ends.at[pl.ds(0, PACK)], ends.at[pl.ds(PACK, PACK)], 0)
    send_out = to_pair(out_own, out_other, 1)
    send_w = [
        to_pair(w_own.at[pl.ds(d * depth, depth)], w_other.at[pl.ds(d * depth, depth)], 2 + d)
        for d in range(DEPTH_PIECES)
    ]
    send_ends.start()
    send_out.start()
    send_w[0].start()
    own_piece(ROW_PIECES - 1)
    send_ends.wait_recv()

    inner = jnp.dot(ends[...], w_own[...], preferred_element_type=jnp.float32)
    active = jnp.tanh(inner).astype(jnp.bfloat16).astype(jnp.float32)
    wide = out_own[...].astype(jnp.float32)
    scale = jnp.concatenate([own_mix[k] * wide[k : k + 1] for k in range(heads)], axis=1)
    part = jnp.sum(active * scale, axis=1, keepdims=True)
    line = lax.broadcasted_iota(jnp.int32, (2 * PACK, lanes), 0)
    lane = lax.broadcasted_iota(jnp.int32, (2 * PACK, lanes), 1)
    mine = (line < count) & (lane == me * count + line)
    theirs = (line >= PACK) & (line < PACK + count) & (
        lane == (4 * chip + 1 - me) * count + line - PACK
    )
    note = jnp.sum(jnp.where(mine | theirs, part, 0.0), axis=0, keepdims=True)
    msg[...] = note
    slots[me] = note

    def tell(step, _):
        other = lax.rem(me + step, devices)
        pltpu.make_async_remote_copy(
            src_ref=msg, dst_ref=slots.at[me], send_sem=all_send, recv_sem=all_recv,
            device_id=(other // 2, lax.rem(other, 2)), device_id_type=MESH,
        ).start()
        return 0

    lax.fori_loop(1, devices, tell, 0)
    for copy in send_w[1:]:
        copy.start()

    send_out.wait_recv()
    other_lhs = reader(out_other)
    for d in range(DEPTH_PIECES):
        send_w[d].wait_recv()
        cut = pl.ds(d * depth, depth)
        for m in range(ROW_PIECES):
            at = pl.ds(m * piece, piece)
            inner = jnp.dot(rows_of(m, cut), w_other[cut, :], preferred_element_type=jnp.float32)
            if d > 0:
                inner = acc[at, :] + inner
            if d < DEPTH_PIECES - 1:
                acc[at, :] = inner
            else:
                comb[:, at] = comb[:, at] + scores(inner, other_lhs, other_mix)

    rest = slots.at[pl.ds(0, devices - 1)]
    pltpu.make_async_copy(rest, rest, all_recv).wait()

    reward = jnp.sum(slots[...], axis=0)[:, : groups_v.shape[1]]
    labels = groups_v[...]
    spot = lax.broadcasted_iota(jnp.int32, reward.shape, 1)
    place = lax.broadcasted_iota(jnp.int32, (1, seq), 1)
    for r in range(count):
        index = me * count + r
        member = labels == groups_s[index]
        own = jnp.sum(jnp.where(spot == index, reward, 0.0), axis=1, keepdims=True)
        mean = jnp.sum(jnp.where(member, reward, 0.0), axis=1, keepdims=True) / GROUP
        gap = reward - mean
        var = jnp.sum(jnp.where(member, gap * gap, 0.0), axis=1, keepdims=True) / GROUP
        best = jnp.max(jnp.where(member, reward, -jnp.inf), axis=1, keepdims=True)
        base = (own - mean) / jnp.sqrt(var + var_offset) - gap_weight * (best - own)
        shaped = base + token_weight * comb[:, pl.ds(r * seq, seq)]
        valid = (place < lens_s[r]) & (mask_v[pl.ds(r, 1), :] == 1)
        out[pl.ds(r, 1), :] = jnp.where(valid, jnp.clip(shaped, -clip_limit, clip_limit), 0.0)

    send_ends.wait_send()
    send_out.wait_send()
    for copy in send_w:
        copy.wait_send()
    pltpu.make_async_copy(rest, rest, all_send).wait()


def solution(mesh):
    chips = mesh.shape["dp"]

    def on_device(hidden, head_proj, head_out, head_ratio, group_of, lengths, token_mask):
        count, seq, width = hidden.shape
        heads, _, rank = head_proj.shape
        everyone = group_of.shape[0]
        lanes = -(-everyone // 128) * 128
        hbm = pl.BlockSpec(memory_space=pltpu.HBM)
        bf16, f32, i32 = jnp.bfloat16, jnp.float32, jnp.int32
        return pl.pallas_call(
            functools.partial(kernel, chips),
            out_shape=jax.ShapeDtypeStruct((count, seq), f32),
            in_specs=[hbm] * 7,
            out_specs=pl.BlockSpec(memory_space=pltpu.VMEM),
            scratch_shapes=[
                pltpu.VMEM((count * seq // PACK, PACK, width), bf16),
                pltpu.VMEM((width, heads * rank), bf16),
                pltpu.VMEM((width, heads * rank), bf16),
                pltpu.VMEM((heads, rank), bf16),
                pltpu.VMEM((heads, rank), bf16),
                pltpu.VMEM((count * seq, heads * rank), f32),
                pltpu.VMEM((1, count * seq), f32),
                pltpu.VMEM((2 * PACK, width), bf16),
                pltpu.VMEM((1, lanes), f32),
                pltpu.VMEM((2 * chips, 1, lanes), f32),
                pltpu.SMEM(head_ratio.shape, i32),
                pltpu.SMEM(group_of.shape, i32),
                pltpu.SMEM(lengths.shape, i32),
                pltpu.VMEM((1, everyone), i32),
                pltpu.VMEM((count, seq), i32),
                pltpu.SemaphoreType.DMA((ROW_PIECES,)),
                pltpu.SemaphoreType.DMA((heads,)),
                pltpu.SemaphoreType.DMA((6,)),
                pltpu.SemaphoreType.DMA((2 + DEPTH_PIECES,)),
                pltpu.SemaphoreType.DMA((2 + DEPTH_PIECES,)),
                pltpu.SemaphoreType.DMA,
                pltpu.SemaphoreType.DMA,
            ],
            compiler_params=pltpu.CompilerParams(
                collective_id=0, has_side_effects=True, vmem_limit_bytes=60 * 1024 * 1024
            ),
            name="advantages",
        )(hidden.reshape(-1, PACK, width), head_proj, head_out, head_ratio, group_of, lengths, token_mask)

    return jax.shard_map(
        on_device,
        mesh=mesh,
        in_specs=(
            P(("dp", "head"), None, None),
            P("head", None, None),
            P("head", None),
            P(),
            P(),
            P(("dp", "head")),
            P(("dp", "head"), None),
        ),
        out_specs=P(("dp", "head"), None),
        check_vma=False,
    )
```

time: 82.4 us -> 20 us (0.24)
  blocking collectives: 42.5 us -> 0 us
  Pallas kernels: 0 us -> 18.5 us
  between operations: 13.4 us -> 0.01 us
  waiting for transfers between devices: 11.9 us -> 0 us
  matrix products: 8.41 us -> 0 us
  other arithmetic: 4.75 us -> 0 us
    unnamed x1 -> x0, blocking collectives: 40.5 us -> none
    pallas_call x0 -> x1, Pallas kernels: none -> 18.5 us  [on_device(): pl.pallas_call(functools.partial(kernel, chips), out_shape=jax.ShapeDtype...]
    all_gather x1 -> x0, waiting for transfers between devices: 11.2 us -> none  [on_device(): lax.all_gather(head_proj, 'head', axis=0, tiled=True)]
    dot_general x1 -> x0, matrix products: 8.41 us -> none  [mixture_scores(): jnp.einsum('htr,hr->ht', active, readout, preferred_element_type=jnp.floa...]
    reduce_sum x7 -> x0, other arithmetic: 2.09 us -> none  [the longest x1 1.26 us: head_mixture(): return ratios / jnp.sum(ratios)]
    all_gather x1 -> x0, blocking collectives: 2.08 us -> none  [on_device(): lax.all_gather(head_out, 'head', axis=0, tiled=True)]
    div x4 -> x0, other arithmetic: 1.32 us -> none  [the longest x1 1.3 us: head_mixture(): return ratios / jnp.sum(ratios)]
    unnamed x8 -> x1, local copies, waits for them, and re-layouts: 0.25 us -> 1.28 us
  transfers between devices with their start and end apart: 1 -> 0, of which waited for: 1 -> 0; matrix products, arithmetic and copies ran while one was open for 5% -> 0% of each run, Pallas kernels for 0% -> 0%
where the time goes in v1:
time: 20 us; the launch traced here: 19.7 us
  Pallas kernels  18.5 us (92%)
  local copies, waits for them, and re-layouts  1.28 us (6%)
    pallas_call x1, Pallas kernels, on_device(): pl.pallas_call(functools.partial(kernel, chips), out_shape=jax.ShapeDtype...  18.5 us
    unnamed x1, local copies, waits for them, and re-layouts  1.28 us

profile of v1, /device:TPU:0, one launch (start us, length us, event | category | flops | bytes accessed | tf_op | source)
XLA Modules:
  0.0 19.7 jit_solution(17494394261189402480)
XLA Ops:
  0.0 18.5 %advantages.1 = f32[2,512]{1,0:T(2,128)} custom-call(bf16[64,16,3584]{2,1,0:T(8,128)(2,1)} %bitcast.1, bf16[2,3584,128]{2,1,0:T(8,128)(2,1)} %proj.1, bf16[2,128]{1,0:T(2,128)(2,1)} %readout.1, s32[4]{0:T(128)} %ratio.1, s32[64]{0:T(128)} %groups.1, s32[2]{0:T(128)} %lens.1, s32[2,512]{1,0:T(2,128)} %mask.1), custom_call_target="tpu_custom_call" | custom-call | tf_op jit(solution)/shard_map/advantages/pallas_call | solution.py:228
  18.5 1.3 %copy.9 = f32[2,512]{1,0:T(2,128)} copy(f32[2,512]{1,0:T(2,128)} %advantages.1) | data formatting | bytes 8192

commit v2 on v1

--- a/solution.py
+++ b/solution.py
@@ -15,7 +15,6 @@
 clip_limit = 2.0
 var_offset = 0.04
 
-ROW_PIECES = 4
 DEPTH_PIECES = 2
 PACK = 16
 
@@ -34,8 +33,6 @@
     devices = 2 * chips
     me = 2 * chip + core
     total_rows = count * seq
-    piece = total_rows // ROW_PIECES
-    blocks = piece // PACK
     depth = width // DEPTH_PIECES
     lanes = msg.shape[1]
 
@@ -49,13 +46,10 @@
         pltpu.make_async_copy(proj.at[k], w_own.at[:, pl.ds(k * rank, rank)], w_sem.at[k])
         for k in range(heads)
     ]
+    cuts = [pl.ds(d * depth, depth) for d in range(DEPTH_PIECES)]
     h_loads = [
-        pltpu.make_async_copy(
-            hidden.at[pl.ds(m * blocks, blocks)],
-            rows_all.at[pl.ds(m * blocks, blocks)],
-            row_sem.at[m],
-        )
-        for m in range(ROW_PIECES)
+        pltpu.make_async_copy(hidden.at[:, :, cuts[d]], rows_all.at[:, :, cuts[d]], row_sem.at[d])
+        for d in range(DEPTH_PIECES)
     ]
     for copy in w_loads + h_loads + loads:
         copy.start()
@@ -104,18 +98,22 @@
 
     own_lhs = reader(out_own)
 
-    def rows_of(m, cut):
-        return rows_all[pl.ds(m * blocks, blocks), :, cut].reshape(piece, -1)
-
-    def own_piece(m):
-        at = pl.ds(m * piece, piece)
-        inner = jnp.dot(rows_of(m, pl.ds(0, width)), w_own[...], preferred_element_type=jnp.float32)
-        comb[:, at] = scores(inner, own_lhs, own_mix)
-
-    for m in range(ROW_PIECES - 1):
-        h_loads[m].wait()
-        own_piece(m)
-    h_loads[ROW_PIECES - 1].wait()
+    def partial(values, d):
+        rows = rows_all[:, :, cuts[d]].reshape(total_rows, depth)
+        return jnp.dot(rows, values[cuts[d], :], preferred_element_type=jnp.float32)
+
+    def add_partial(values, d):
+        inner = partial(values, d)
+        if d > 0:
+            inner = acc[...] + inner
+        if d < DEPTH_PIECES - 1:
+            acc[...] = inner
+        return inner
+
+    for d in range(DEPTH_PIECES - 1):
+        h_loads[d].wait()
+        add_partial(w_own, d)
+    h_loads[DEPTH_PIECES - 1].wait()
 
     sub = lax.broadcasted_iota(jnp.int32, (PACK, width), 0)
     picked = jnp.zeros((PACK, width), jnp.float32)
@@ -137,13 +135,13 @@
     send_ends = to_pair(ends.at[pl.ds(0, PACK)], ends.at[pl.ds(PACK, PACK)], 0)
     send_out = to_pair(out_own, out_other, 1)
     send_w = [
-        to_pair(w_own.at[pl.ds(d * depth, depth)], w_other.at[pl.ds(d * depth, depth)], 2 + d)
+        to_pair(w_own.at[cuts[d]], w_other.at[cuts[d]], 2 + d)
         for d in range(DEPTH_PIECES)
     ]
     send_ends.start()
     send_out.start()
     send_w[0].start()
-    own_piece(ROW_PIECES - 1)
+    comb[...] = scores(add_partial(w_own, DEPTH_PIECES - 1), own_lhs, own_mix)
     send_ends.wait_recv()
 
     inner = jnp.dot(ends[...], w_own[...], preferred_element_type=jnp.float32)
@@ -177,16 +175,8 @@
     other_lhs = reader(out_other)
     for d in range(DEPTH_PIECES):
         send_w[d].wait_recv()
-        cut = pl.ds(d * depth, depth)
-        for m in range(ROW_PIECES):
-            at = pl.ds(m * piece, piece)
-            inner = jnp.dot(rows_of(m, cut), w_other[cut, :], preferred_element_type=jnp.float32)
-            if d > 0:
-                inner = acc[at, :] + inner
-            if d < DEPTH_PIECES - 1:
-                acc[at, :] = inner
-            else:
-                comb[:, at] = comb[:, at] + scores(inner, other_lhs, other_mix)
+        inner = add_partial(w_other, d)
+    comb[...] = comb[...] + scores(inner, other_lhs, other_mix)
 
     rest = slots.at[pl.ds(0, devices - 1)]
     pltpu.make_async_copy(rest, rest, all_recv).wait()
@@ -246,7 +236,7 @@
                 pltpu.SMEM(lengths.shape, i32),
                 pltpu.VMEM((1, everyone), i32),
                 pltpu.VMEM((count, seq), i32),
-                pltpu.SemaphoreType.DMA((ROW_PIECES,)),
+                pltpu.SemaphoreType.DMA((DEPTH_PIECES,)),
                 pltpu.SemaphoreType.DMA((heads,)),
                 pltpu.SemaphoreType.DMA((6,)),
                 pltpu.SemaphoreType.DMA((2 + DEPTH_PIECES,)),

time: 20 us -> 19.3 us (0.965)
  Pallas kernels: 18.5 us -> 17.8 us
    pallas_call x1, Pallas kernels: 18.5 us -> 17.8 us  [on_device(): pl.pallas_call(functools.partial(kernel, chips), out_shape=jax.ShapeDtype...]
where the time goes in v2:
time: 19.3 us; the launch traced here: 19.1 us
  Pallas kernels  17.8 us (92%)
  local copies, waits for them, and re-layouts  1.28 us (7%)
    pallas_call x1, Pallas kernels, on_device(): pl.pallas_call(functools.partial(kernel, chips), out_shape=jax.ShapeDtype...  17.8 us
    unnamed x1, local copies, waits for them, and re-layouts  1.28 us

profile of v2, /device:TPU:0, one launch (start us, length us, event | category | flops | bytes accessed | tf_op | source)
XLA Modules:
  0.0 19.1 jit_solution(3706195907248879623)
XLA Ops:
  0.0 17.8 %advantages.1 = f32[2,512]{1,0:T(2,128)} custom-call(bf16[64,16,3584]{2,1,0:T(8,128)(2,1)} %bitcast.1, bf16[2,3584,128]{2,1,0:T(8,128)(2,1)} %proj.1, bf16[2,128]{1,0:T(2,128)(2,1)} %readout.1, s32[4]{0:T(128)} %ratio.1, s32[64]{0:T(128)} %groups.1, s32[2]{0:T(128)} %lens.1, s32[2,512]{1,0:T(2,128)} %mask.1), custom_call_target="tpu_custom_call" | custom-call | tf_op jit(solution)/shard_map/advantages/pallas_call | solution.py:218
  17.8 1.3 %copy.9 = f32[2,512]{1,0:T(2,128)} copy(f32[2,512]{1,0:T(2,128)} %advantages.1) | data formatting | bytes 8192

commit v3 on v2

--- a/solution.py
+++ b/solution.py
@@ -51,22 +51,60 @@
         pltpu.make_async_copy(hidden.at[:, :, cuts[d]], rows_all.at[:, :, cuts[d]], row_sem.at[d])
         for d in range(DEPTH_PIECES)
     ]
-    for copy in w_loads + h_loads + loads:
+    for copy in loads[:1] + h_loads + w_loads + loads[1:]:
         copy.start()
 
     barrier = pltpu.get_barrier_semaphore()
 
-    def greet(step, _):
-        other = lax.rem(me + step, devices)
-        pl.semaphore_signal(
-            barrier, inc=1, device_id=(other // 2, lax.rem(other, 2)), device_id_type=MESH
+    def each_other(act):
+        def both(step, _):
+            there = lax.rem(chip + step, chips)
+            act((there, core))
+            act((there, 1 - core))
+            return 0
+
+        if chips <= 16:
+            for step in range(1, chips):
+                both(step, 0)
+        else:
+            lax.fori_loop(1, chips, both, 0)
+        act((chip, 1 - core))
+
+    each_other(
+        lambda place: pl.semaphore_signal(barrier, inc=1, device_id=place, device_id_type=MESH)
+    )
+
+    for copy in loads[:1] + h_loads:
+        copy.wait()
+
+    sub = lax.broadcasted_iota(jnp.int32, (PACK, width), 0)
+    picked = jnp.zeros((PACK, width), jnp.float32)
+    for r in range(count):
+        last = lens_s[r] - 1
+        block = rows_all[r * (seq // PACK) + lax.div(last, PACK)].astype(jnp.float32)
+        row = jnp.sum(jnp.where(sub == lax.rem(last, PACK), block, 0.0), axis=0, keepdims=True)
+        picked = jnp.where(sub == r, jnp.broadcast_to(row, (PACK, width)), picked)
+    ends[pl.ds(0, PACK), :] = picked.astype(jnp.bfloat16)
+
+    pl.semaphore_wait(barrier, devices - 1)
+
+    def to_pair(src, dst, k):
+        return pltpu.make_async_remote_copy(
+            src_ref=src, dst_ref=dst, send_sem=pair_send.at[k], recv_sem=pair_recv.at[k],
+            device_id=(chip, 1 - core), device_id_type=MESH,
         )
-        return 0
-
-    lax.fori_loop(1, devices, greet, 0)
-
-    for copy in loads + w_loads:
+
+    send_ends = to_pair(ends.at[pl.ds(0, PACK)], ends.at[pl.ds(PACK, PACK)], 0)
+    send_out = to_pair(out_own, out_other, 1)
+    send_w = [
+        to_pair(w_own.at[cuts[d]], w_other.at[cuts[d]], 2 + d)
+        for d in range(DEPTH_PIECES)
+    ]
+    send_ends.start()
+    for copy in w_loads + loads[1:]:
         copy.wait()
+    send_out.start()
+    send_w[0].start()
 
     weights = [ratio_s[k].astype(jnp.float32) for k in range(2 * heads)]
     weight_sum = sum(weights[1:], weights[0])
@@ -110,38 +148,7 @@
             acc[...] = inner
         return inner
 
-    for d in range(DEPTH_PIECES - 1):
-        h_loads[d].wait()
-        add_partial(w_own, d)
-    h_loads[DEPTH_PIECES - 1].wait()
-
-    sub = lax.broadcasted_iota(jnp.int32, (PACK, width), 0)
-    picked = jnp.zeros((PACK, width), jnp.float32)
-    for r in range(count):
-        last = lens_s[r] - 1
-        block = rows_all[r * (seq // PACK) + lax.div(last, PACK)].astype(jnp.float32)
-        row = jnp.sum(jnp.where(sub == lax.rem(last, PACK), block, 0.0), axis=0, keepdims=True)
-        picked = jnp.where(sub == r, jnp.broadcast_to(row, (PACK, width)), picked)
-    ends[pl.ds(0, PACK), :] = picked.astype(jnp.bfloat16)
-
-    pl.semaphore_wait(barrier, devices - 1)
-
-    def to_pair(src, dst, k):
-        return pltpu.make_async_remote_copy(
-            src_ref=src, dst_ref=dst, send_sem=pair_send.at[k], recv_sem=pair_recv.at[k],
-            device_id=(chip, 1 - core), device_id_type=MESH,
-        )
-
-    send_ends = to_pair(ends.at[pl.ds(0, PACK)], ends.at[pl.ds(PACK, PACK)], 0)
-    send_out = to_pair(out_own, out_other, 1)
-    send_w = [
-        to_pair(w_own.at[cuts[d]], w_other.at[cuts[d]], 2 + d)
-        for d in range(DEPTH_PIECES)
-    ]
-    send_ends.start()
-    send_out.start()
-    send_w[0].start()
-    comb[...] = scores(add_partial(w_own, DEPTH_PIECES - 1), own_lhs, own_mix)
+    add_partial(w_own, 0)
     send_ends.wait_recv()
 
     inner = jnp.dot(ends[...], w_own[...], preferred_element_type=jnp.float32)
@@ -159,17 +166,18 @@
     msg[...] = note
     slots[me] = note
 
-    def tell(step, _):
-        other = lax.rem(me + step, devices)
-        pltpu.make_async_remote_copy(
+    each_other(
+        lambda place: pltpu.make_async_remote_copy(
             src_ref=msg, dst_ref=slots.at[me], send_sem=all_send, recv_sem=all_recv,
-            device_id=(other // 2, lax.rem(other, 2)), device_id_type=MESH,
+            device_id=place, device_id_type=MESH,
         ).start()
-        return 0
-
-    lax.fori_loop(1, devices, tell, 0)
+    )
     for copy in send_w[1:]:
         copy.start()
+
+    for d in range(1, DEPTH_PIECES):
+        inner = add_partial(w_own, d)
+    comb[...] = scores(inner, own_lhs, own_mix)
 
     send_out.wait_recv()
     other_lhs = reader(out_other)
@@ -183,20 +191,29 @@
 
     reward = jnp.sum(slots[...], axis=0)[:, : groups_v.shape[1]]
     labels = groups_v[...]
-    spot = lax.broadcasted_iota(jnp.int32, reward.shape, 1)
-    place = lax.broadcasted_iota(jnp.int32, (1, seq), 1)
+    shape = (count, reward.shape[1])
+    rollout = lax.broadcasted_iota(jnp.int32, shape, 0)
+    lane_of = lax.broadcasted_iota(jnp.int32, shape, 1)
+    wide = jnp.broadcast_to(reward, shape)
+    group = jnp.zeros(shape, jnp.int32)
+    length = jnp.zeros((count, seq), jnp.int32)
+    line = lax.broadcasted_iota(jnp.int32, (count, seq), 0)
     for r in range(count):
-        index = me * count + r
-        member = labels == groups_s[index]
-        own = jnp.sum(jnp.where(spot == index, reward, 0.0), axis=1, keepdims=True)
-        mean = jnp.sum(jnp.where(member, reward, 0.0), axis=1, keepdims=True) / GROUP
-        gap = reward - mean
-        var = jnp.sum(jnp.where(member, gap * gap, 0.0), axis=1, keepdims=True) / GROUP
-        best = jnp.max(jnp.where(member, reward, -jnp.inf), axis=1, keepdims=True)
-        base = (own - mean) / jnp.sqrt(var + var_offset) - gap_weight * (best - own)
-        shaped = base + token_weight * comb[:, pl.ds(r * seq, seq)]
-        valid = (place < lens_s[r]) & (mask_v[pl.ds(r, 1), :] == 1)
-        out[pl.ds(r, 1), :] = jnp.where(valid, jnp.clip(shaped, -clip_limit, clip_limit), 0.0)
+        group = jnp.where(rollout == r, groups_s[me * count + r], group)
+        length = jnp.where(line == r, lens_s[r], length)
+    member = jnp.broadcast_to(labels, shape) == group
+    own = jnp.sum(jnp.where(lane_of == me * count + rollout, wide, 0.0), axis=1, keepdims=True)
+    mean = jnp.sum(jnp.where(member, wide, 0.0), axis=1, keepdims=True) / GROUP
+    gap = wide - mean
+    var = jnp.sum(jnp.where(member, gap * gap, 0.0), axis=1, keepdims=True) / GROUP
+    best = jnp.max(jnp.where(member, wide, -jnp.inf), axis=1, keepdims=True)
+    base = (own - mean) / jnp.sqrt(var + var_offset) - gap_weight * (best - own)
+    shaped = base + token_weight * jnp.concatenate(
+        [comb[:, pl.ds(r * seq, seq)] for r in range(count)], axis=0
+    )
+    place = lax.broadcasted_iota(jnp.int32, (count, seq), 1)
+    valid = (place < length) & (mask_v[...] == 1)
+    out[...] = jnp.where(valid, jnp.clip(shaped, -clip_limit, clip_limit), 0.0)
 
     send_ends.wait_send()
     send_out.wait_send()

time: 19.3 us -> 18.1 us (0.938)
  Pallas kernels: 17.8 us -> 16.6 us
    pallas_call x1, Pallas kernels: 17.8 us -> 16.6 us  [on_device(): pl.pallas_call(functools.partial(kernel, chips), out_shape=jax.ShapeDtype...]
where the time goes in v3:
time: 18.1 us; the launch traced here: 17.9 us
  Pallas kernels  16.6 us (92%)
  local copies, waits for them, and re-layouts  1.28 us (7%)
    pallas_call x1, Pallas kernels, on_device(): pl.pallas_call(functools.partial(kernel, chips), out_shape=jax.ShapeDtype...  16.6 us
    unnamed x1, local copies, waits for them, and re-layouts  1.28 us

profile of v3, /device:TPU:0, one launch (start us, length us, event | category | flops | bytes accessed | tf_op | source)
XLA Modules:
  0.0 17.9 jit_solution(9065194966350801919)
XLA Ops:
  0.0 16.6 %advantages.1 = f32[2,512]{1,0:T(2,128)} custom-call(bf16[64,16,3584]{2,1,0:T(8,128)(2,1)} %bitcast.1, bf16[2,3584,128]{2,1,0:T(8,128)(2,1)} %proj.1, bf16[2,128]{1,0:T(2,128)(2,1)} %readout.1, s32[4]{0:T(128)} %ratio.1, s32[64]{0:T(128)} %groups.1, s32[2]{0:T(128)} %lens.1, s32[2,512]{1,0:T(2,128)} %mask.1), custom_call_target="tpu_custom_call" | custom-call | tf_op jit(solution)/shard_map/advantages/pallas_call | solution.py:235
  16.6 1.3 %copy.9 = f32[2,512]{1,0:T(2,128)} copy(f32[2,512]{1,0:T(2,128)} %advantages.1) | data formatting | bytes 8192
